TPU v7x, 32 devices: a whole 2x2x4 slice. The times are simulated.
32 devices in a mesh: groups: 2 (over y), fibre: 4 (over z), seg: 2 (over x), rec: 2 (over core).
Axes of the slice: x: 2, y: 2, z: 4, core: 2. Of those that a mesh axis runs over, the one named last changes fastest.
Arguments:
- records: bfloat16 [2, 2048, 1024], P('rec', 'fibre', ('groups', 'seg')), parts along dimension 2, may hold values from -6 to 6
- pairs: int32 [16, 2], replicated, may hold values from 0 to 15
- observed: float32 [32, 32, 256], P(('groups', 'fibre', 'seg')), parts along dimension 0, may hold values from -6 to 6
- lag_mask: int32 [32, 256], P(('groups', 'fibre', 'seg')), parts along dimension 0, may hold values 0 or 1
Outputs:
- adjoint_sources: bfloat16 [2, 2048, 1024], P('rec', 'fibre', ('groups', 'seg')), parts along dimension 2
There are 2 independent parts, one for each index of `groups`. A program takes and returns all parts, laid end to end along the dimension named above; an argument that names none is the same for every part. Nothing has to cross between parts.
All inputs are finite; a program needn't handle non-finite values. No bound on the sum of `lag_mask` on one device may be relied on, other than what follows from the above.
Results may differ from a plain program's by a relative error of at most 0.015.
Values may be sent and summed in bfloat16 or wider, within the bound.
A program may use at most 64 MiB of HBM per device.

v0:
```python
import jax
import jax.numpy as jnp
from jax import lax
from jax.sharding import PartitionSpec as P

S = 2048
F = 1024
LAGS = 256
BLOCK = 32
CH_DEV = 64


def forward_table():
    freq_index = jnp.arange(F, dtype=jnp.int32)
    time_index = jnp.arange(S, dtype=jnp.int32)
    phase = freq_index[:, None] * time_index[None, :] % S
    angles = phase.astype(jnp.float32) * (2.0 * jnp.pi / S)
    scale = 1.0 / jnp.sqrt(jnp.float32(S))
    return jnp.stack(
        [
            (jnp.cos(angles) * scale).astype(jnp.bfloat16),
            (-jnp.sin(angles) * scale).astype(jnp.bfloat16),
        ],
        axis=1,
    )


def lag_table():
    freq_index = jnp.arange(F, dtype=jnp.int32)
    shifts = (jnp.arange(LAGS, dtype=jnp.int32) - LAGS // 2) % S
    phase = freq_index[:, None] * shifts[None, :] % S
    angles = phase.astype(jnp.float32) * (2.0 * jnp.pi / S)
    scale = 1.0 / jnp.sqrt(jnp.float32(F))
    return jnp.stack(
        [
            (jnp.cos(angles) * scale).astype(jnp.bfloat16),
            (-jnp.sin(angles) * scale).astype(jnp.bfloat16),
        ],
        axis=1,
    )


def synthesize(incoming, table):
    count = incoming.shape[-1]
    flat = incoming.reshape(2 * F, count)
    result = jnp.einsum(
        "qn,qt->tn", flat, table.reshape(2 * F, S), preferred_element_type=jnp.float32
    )
    return result.astype(jnp.bfloat16)


def on_device(records, pairs, observed, lag_mask):
    fibre_count = lax.axis_size("fibre")
    seg_count = lax.axis_size("seg")
    spread_count = fibre_count * seg_count
    freq_dev = F // spread_count
    blocks_dev = CH_DEV // BLOCK
    block_count = CH_DEV * spread_count // BLOCK
    pair_total = pairs.shape[0]
    pairs_dev = pair_total // spread_count
    table = forward_table()
    lags = lag_table()
    spans = records.reshape(1, S // fibre_count, fibre_count, CH_DEV)
    incoming = lax.all_to_all(spans, "fibre", split_axis=2, concat_axis=1, tiled=True)
    count = incoming.shape[3]
    signal = incoming.reshape(S, count)
    result = jnp.einsum(
        "qs,sn->qn", table.reshape(2 * F, S), signal, preferred_element_type=jnp.float32
    )
    spectra = result.reshape(F, 2, count).astype(jnp.bfloat16)
    widened = lax.all_to_all(spectra, ("fibre", "seg"), split_axis=0, concat_axis=2, tiled=True)
    seg_blocks = fibre_count * blocks_dev
    slot_ids = (
        pairs % seg_blocks // blocks_dev * seg_count + pairs // seg_blocks
    ) * blocks_dev + pairs % blocks_dev
    blocks_grid = widened.reshape(freq_dev, 2, block_count, BLOCK)
    first_side = jnp.take(blocks_grid, slot_ids[:, 0], axis=2).astype(jnp.float32)
    second_side = jnp.take(blocks_grid, slot_ids[:, 1], axis=2).astype(jnp.float32)
    first_re, first_im = (first_side[:, 0], first_side[:, 1])
    second_re, second_im = (second_side[:, 0], second_side[:, 1])
    cross_re = first_re * second_re + first_im * second_im
    cross_im = first_im * second_re - first_re * second_im
    cross_spec = jnp.stack([cross_re, cross_im], axis=1).astype(jnp.bfloat16)
    cross_spec = cross_spec.reshape(freq_dev, 2, spread_count, pairs_dev * BLOCK)
    owned_spec = lax.all_to_all(
        cross_spec, ("fibre", "seg"), split_axis=2, concat_axis=0, tiled=True
    )
    owned_spec = owned_spec.reshape(F, 2, pairs_dev * BLOCK)
    partial_corr = jnp.einsum("wpx,wpl->xl", owned_spec, lags, preferred_element_type=jnp.float32)
    synthetic = (
        lax.psum(partial_corr.astype(jnp.bfloat16), "rec")
        .astype(jnp.float32)
        .reshape(pairs_dev, BLOCK, LAGS)
    )
    weights = lag_mask[:, None, :].astype(jnp.float32) * jnp.tanh(synthetic - observed)
    weights_low = weights.astype(jnp.bfloat16).reshape(pairs_dev * BLOCK, LAGS)
    adjoint_spec = jnp.einsum("xl,wpl->wpx", weights_low, lags, preferred_element_type=jnp.float32)
    adjoint_spec = adjoint_spec.astype(jnp.bfloat16).reshape(F, 2, 1, pairs_dev * BLOCK)
    returned = lax.all_to_all(
        adjoint_spec, ("fibre", "seg"), split_axis=0, concat_axis=2, tiled=True
    )
    returned = returned.reshape(freq_dev, 2, pair_total, BLOCK).astype(jnp.float32)
    adjoint_re, adjoint_im = (returned[:, 0], returned[:, 1])
    grad_first = jnp.stack(
        [
            adjoint_re * second_re - adjoint_im * second_im,
            adjoint_re * second_im + adjoint_im * second_re,
        ],
        axis=1,
    )
    grad_second = jnp.stack(
        [
            adjoint_re * first_re + adjoint_im * first_im,
            adjoint_re * first_im - adjoint_im * first_re,
        ],
        axis=1,
    )
    contributions = jnp.concatenate([grad_first, grad_second], axis=2)
    endpoint_ids = jnp.concatenate([slot_ids[:, 0], slot_ids[:, 1]])
    summed = jax.ops.segment_sum(
        jnp.moveaxis(contributions, 2, 0), endpoint_ids, num_segments=block_count
    )
    block_adjoint = jnp.moveaxis(summed, 0, 2).astype(jnp.bfloat16)
    outgoing = block_adjoint.reshape(freq_dev, 2, spread_count, CH_DEV)
    sources = synthesize(
        lax.all_to_all(outgoing, ("fibre", "seg"), split_axis=2, concat_axis=0, tiled=True), table
    )
    regrouped = lax.all_to_all(sources, "fibre", split_axis=0, concat_axis=1, tiled=True)
    return regrouped[None]


def solution(mesh):
    in_specs = (
        P("rec", "fibre", ("groups", "seg")),
        P(),
        P(("groups", "fibre", "seg"), None, None),
        P(("groups", "fibre", "seg"), None),
    )
    out_specs = P("rec", "fibre", ("groups", "seg"))
    return jax.shard_map(
        on_device, mesh=mesh, in_specs=in_specs, out_specs=out_specs, check_vma=False
    )
```

profile of v0, /device:TPU:0, one launch (start us, length us, event | category | flops | bytes accessed | tf_op | source)
XLA Modules:
  0.0 163.2 jit_solution(8597783628842389983)
XLA Ops:
  0.0 1.8 %copy.59 = bf16[1,512,256]{1,2,0:T(8,128)(2,1)} copy(bf16[1,512,256]{2,1,0:T(8,128)(2,1)} %param.6) | data formatting | bytes 524288 | tf_op args[0]
  1.8 6.3 %all-to-all-start = ((bf16[1,512,4,64]{1,3,0,2:T(8,128)(2,1)}), bf16[1,512,4,64]{1,3,0,2:T(8,128)(2,1)S(1)}, u32[]{:S(2)}, u32[]{:S(2)}) async-start(bf16[1,512,4,64]{1,3,0,2:T(8,128)(2,1)} %bitcast.3), calls=%async_computation | async-start | bytes 524288 | tf_op jit(solution)/shard_map/all_to_all | solution.py:64
  8.1 35.0 %multiply_convert_fusion = (bf16[1024,1,2048]{2,0,1:T(8,128)(2,1)}, bf16[1024,1,2048]{2,0,1:T(8,128)(2,1)}) fusion(), kind=kLoop, calls=%fused_computation.10 | loop fusion | flops 39845888 | bytes 8388608 | tf_op jit(solution)/shard_map/convert_element_type | solution.py:22
  43.6 5.1 %convolution_convert_fusion.1 = bf16[1024,2,64]{0,2,1:T(8,128)(2,1)S(1)} fusion(bf16[2048,64,1]{0,1,2:T(8,128)(2,1)S(1)} %reshape.311, bf16[1024,1,2048]{2,0,1:T(8,128)(2,1)} %get-tuple-element.24, bf16[1024,1,2048]{2,0,1:T(8,128)(2,1)} %get-tuple-element.25), kind=kOutput, calls=%fused_computation.19 | convolution fusion | flops 541196288 | bytes 8912896 | tf_op jit(solution)/shard_map/qs,sn->qn/dot_general | solution.py:67
  49.1 1.1 reshape.316
  50.2 6.0 %all-to-all-start.1 = ((bf16[8,2,8192]{2,1,0:T(2,128)(2,1)}), bf16[8,2,8192]{2,1,0:T(2,128)(2,1)S(1)}, u32[]{:S(2)}, u32[]{:S(2)}) async-start(bf16[8,2,8192]{2,1,0:T(2,128)(2,1)} %reshape.316), calls=%async_computation.1 | async-start | bytes 524288 | tf_op jit(solution)/shard_map/all_to_all | solution.py:71
  56.3 8.4 %all-to-all-done.1 = bf16[8,2,8192]{2,1,0:T(2,128)(2,1)S(1)} async-done(((bf16[8,2,8192]{2,1,0:T(2,128)(2,1)}), bf16[8,2,8192]{2,1,0:T(2,128)(2,1)S(1)}, u32[]{:S(2)}, u32[]{:S(2)}) %all-to-all-start.1) | async-done | bytes 262176 | tf_op jit(solution)/shard_map/all_to_all | solution.py:71
  67.0 0.7 pad_maximum_fusion.4
  67.8 3.4 %all-to-all-start.2 = ((bf16[128,2,8,64]{0,3,1,2:T(8,128)(2,1)}), bf16[128,2,8,64]{0,3,1,2:T(8,128)(2,1)S(1)}, u32[]{:S(2)}, u32[]{:S(2)}) async-start(bf16[128,2,8,64]{0,3,1,2:T(8,128)(2,1)} %pad_maximum_fusion.4), calls=%async_computation.2 | async-start | bytes 524288 | tf_op jit(solution)/shard_map/all_to_all | solution.py:85
  71.2 4.5 %multiply_convert_fusion.3 = (bf16[1024,1,256]{2,0,1:T(8,128)(2,1)S(1)}, bf16[1024,1,256]{2,0,1:T(8,128)(2,1)S(1)}) fusion(s32[256]{0:T(256)S(1)} %and_select_fusion), kind=kLoop, calls=%fused_computation.30 | loop fusion | flops 4980736 | bytes 1049600 | tf_op jit(solution)/shard_map/convert_element_type | solution.py:36
  75.7 4.0 %all-to-all-done.2 = bf16[128,2,8,64]{0,3,1,2:T(8,128)(2,1)S(1)} async-done(((bf16[128,2,8,64]{0,3,1,2:T(8,128)(2,1)}), bf16[128,2,8,64]{0,3,1,2:T(8,128)(2,1)S(1)}, u32[]{:S(2)}, u32[]{:S(2)}) %all-to-all-start.2) | async-done | bytes 262176 | tf_op jit(solution)/shard_map/all_to_all | solution.py:85
  80.3 3.4 %psum.7 = bf16[2,32,256]{2,1,0:T(8,128)(2,1)S(1)} all-reduce(bf16[2,32,256]{2,1,0:T(8,128)(2,1)S(1)} %bitcast.121), channel_id=1, replica_groups=mesh['groups'=2,'fibre'=4,'seg'=2,'rec'=2] {'rec'}, use_global_device_ids=true, to_apply=%region_0.2 | all-reduce | flops 16384 | bytes 65536 | tf_op jit(solution)/shard_map/psum | solution.py:91
  84.6 1.1 reshape.318
  85.7 3.6 %all-to-all-start.3 = ((bf16[8,2,8192]{2,1,0:T(2,128)(2,1)}), bf16[8,2,8192]{2,1,0:T(2,128)(2,1)S(1)}, u32[]{:S(2)}, u32[]{:S(2)}) async-start(bf16[8,2,8192]{2,1,0:T(2,128)(2,1)} %reshape.318), calls=%async_computation.3 | async-start | bytes 524288 | tf_op jit(solution)/shard_map/all_to_all | solution.py:99
  89.3 9.4 %all-to-all-done.3 = bf16[8,2,8192]{2,1,0:T(2,128)(2,1)S(1)} async-done(((bf16[8,2,8192]{2,1,0:T(2,128)(2,1)}), bf16[8,2,8192]{2,1,0:T(2,128)(2,1)S(1)}, u32[]{:S(2)}, u32[]{:S(2)}) %all-to-all-start.3) | async-done | bytes 262176 | tf_op jit(solution)/shard_map/all_to_all | solution.py:99
  100.1 2.1 %scatter_fusion = f32[16,128,2,32]{1,3,2,0:T(8,128)S(1)} fusion(f32[16,128,2,32]{1,3,2,0:T(8,128)S(1)} %broadcast_in_dim.23, s32[32]{0:T(128)S(1)} %pad_add_fusion, f32[32,128,2,32]{1,3,2,0:T(8,128)S(1)} %maximum_bitcast_fusion), kind=kCustom, calls=%fused_computation.2 | custom fusion | flops 262144 | bytes 3145856 | tf_op jit(solution)/shard_map/scatter-add | solution.py:120
  102.3 0.7 copy.74
  103.1 3.6 %all-to-all-start.4 = ((bf16[128,2,8,64]{0,3,1,2:T(8,128)(2,1)}), bf16[128,2,8,64]{0,3,1,2:T(8,128)(2,1)S(1)}, u32[]{:S(2)}, u32[]{:S(2)}) async-start(bf16[128,2,8,64]{0,3,1,2:T(8,128)(2,1)} %copy.74), calls=%async_computation.4 | async-start | bytes 524288 | tf_op jit(solution)/shard_map/all_to_all | solution.py:126
  106.7 7.5 %pad_maximum_fusion = bf16[1024,2,2048]{2,0,1:T(8,128)(2,1)} fusion(bf16[1024,1,2048]{2,0,1:T(8,128)(2,1)} %get-tuple-element.24, bf16[1024,1,2048]{2,0,1:T(8,128)(2,1)} %get-tuple-element.25), kind=kLoop, calls=%fused_computation.9 | loop fusion | flops 4194304 | bytes 16777216 | tf_op jit(solution)/shard_map/stack | solution.py:19
  114.1 16.4 %copy.58 = bf16[1024,2,2048]{2,1,0:T(2,128)(2,1)} copy(bf16[1024,2,2048]{2,0,1:T(8,128)(2,1)} %pad_maximum_fusion) | data formatting | bytes 16777216 | tf_op jit(solution)/shard_map/stack | solution.py:19
  130.5 13.1 %reshape.267 = bf16[2048,2048]{1,0:T(8,128)(2,1)} reshape(bf16[1024,2,2048]{2,1,0:T(2,128)(2,1)} %copy.58) | data formatting | bytes 16777216 | tf_op jit(solution)/shard_map/reshape | solution.py:47
  144.0 5.0 %convolution_convert_fusion = bf16[2048,64]{0,1:T(8,128)(2,1)S(1)} fusion(bf16[2048,2048]{1,0:T(8,128)(2,1)} %reshape.267, bf16[2048,64]{1,0:T(8,128)(2,1)S(1)} %bitcast.106), kind=kOutput, calls=%fused_computation.15 | convolution fusion | flops 537001984 | bytes 8912896 | tf_op jit(solution)/shard_map/qn,qt->tn/dot_general | solution.py:46
  149.1 13.3 %all_to_all.85 = bf16[4,512,64]{1,2,0:T(8,128)(2,1)S(1)} all-to-all(bf16[4,512,64]{1,2,0:T(8,128)(2,1)S(1)} %bitcast.117), channel_id=1, replica_groups=mesh['groups'=2,'fibre'=4,'seg'=2,'rec'=2] {'fibre'}, dimensions={0} | all-to-all | bytes 524288 | tf_op jit(solution)/shard_map/all_to_all | solution.py:128
  162.3 0.8 copy.77
  (43 shorter events, 6.4 us)
Async XLA Ops:
  1.8 41.4 %all-to-all-start = ((bf16[1,512,4,64]{1,3,0,2:T(8,128)(2,1)}), bf16[1,512,4,64]{1,3,0,2:T(8,128)(2,1)S(1)}, u32[]{:S(2)}, u32[]{:S(2)}) async-start(bf16[1,512,4,64]{1,3,0,2:T(8,128)(2,1)} %bitcast.3), calls=%async_computation | async-start | bytes 524288 | tf_op jit(solution)/shard_map/all_to_all | solution.py:64
  43.6 12.6 %copy-start.2 = (s32[16,2]{0,1:T(2,128)S(1)}, s32[16,2]{0,1:T(2,128)}, u32[]{:S(2)}) copy-start(s32[16,2]{0,1:T(2,128)} %param.7) | copy-start | bytes 388
  48.7 22.5 %copy-start.1 = (s32[2,256]{1,0:T(2,128)S(1)}, s32[2,256]{1,0:T(2,128)}, u32[]{:S(2)}) copy-start(s32[2,256]{1,0:T(2,128)} %param.9) | copy-start | bytes 6148
  48.7 35.0 %copy-start = (f32[2,32,256]{2,1,0:T(8,128)S(1)}, f32[2,32,256]{2,1,0:T(8,128)}, u32[]{:S(2)}) copy-start(f32[2,32,256]{2,1,0:T(8,128)} %param.8) | copy-start | bytes 196612
  50.2 14.5 %all-to-all-start.1 = ((bf16[8,2,8192]{2,1,0:T(2,128)(2,1)}), bf16[8,2,8192]{2,1,0:T(2,128)(2,1)S(1)}, u32[]{:S(2)}, u32[]{:S(2)}) async-start(bf16[8,2,8192]{2,1,0:T(2,128)(2,1)} %reshape.316), calls=%async_computation.1 | async-start | bytes 524288 | tf_op jit(solution)/shard_map/all_to_all | solution.py:71
  67.8 12.0 %all-to-all-start.2 = ((bf16[128,2,8,64]{0,3,1,2:T(8,128)(2,1)}), bf16[128,2,8,64]{0,3,1,2:T(8,128)(2,1)S(1)}, u32[]{:S(2)}, u32[]{:S(2)}) async-start(bf16[128,2,8,64]{0,3,1,2:T(8,128)(2,1)} %pad_maximum_fusion.4), calls=%async_computation.2 | async-start | bytes 524288 | tf_op jit(solution)/shard_map/all_to_all | solution.py:85
  85.7 13.1 %all-to-all-start.3 = ((bf16[8,2,8192]{2,1,0:T(2,128)(2,1)}), bf16[8,2,8192]{2,1,0:T(2,128)(2,1)S(1)}, u32[]{:S(2)}, u32[]{:S(2)}) async-start(bf16[8,2,8192]{2,1,0:T(2,128)(2,1)} %reshape.318), calls=%async_computation.3 | async-start | bytes 524288 | tf_op jit(solution)/shard_map/all_to_all | solution.py:99
  103.1 40.6 %all-to-all-start.4 = ((bf16[128,2,8,64]{0,3,1,2:T(8,128)(2,1)}), bf16[128,2,8,64]{0,3,1,2:T(8,128)(2,1)S(1)}, u32[]{:S(2)}, u32[]{:S(2)}) async-start(bf16[128,2,8,64]{0,3,1,2:T(8,128)(2,1)} %copy.74), calls=%async_computation.4 | async-start | bytes 524288 | tf_op jit(solution)/shard_map/all_to_all | solution.py:126
where the time goes:
time: 164 us; the launch traced here: 163 us
  other arithmetic  50.7 us (31%)
  local copies, waits for them, and re-layouts  39.9 us (24%)
  starting transfers between devices  23 us (14%)
  waiting for transfers between devices  21.9 us (13%)
  blocking collectives  16.7 us (10%)
  matrix products  10.8 us (7%)
    convert_element_type x1, other arithmetic, forward_table(): (-jnp.sin(angles) * scale).astype(jnp.bfloat16)  35 us
    another operation x1, local copies, waits for them, and re-layouts, forward_table(): jnp.stack([(jnp.cos(angles) * scale).astype(jnp.bfloat16), (-jnp.sin(angl...  16.4 us
    all_to_all x1, blocking collectives, on_device(): lax.all_to_all(sources, 'fibre', split_axis=0, concat_axis=1, tiled=True)  13.3 us
    reshape x1, local copies, waits for them, and re-layouts, synthesize(): table.reshape(2 * F, S)  13.1 us
    all_to_all x1, waiting for transfers between devices, on_device(): lax.all_to_all(adjoint_spec, ('fibre', 'seg'), split_axis=0, concat_axis=...  9.42 us
    all_to_all x1, waiting for transfers between devices, on_device(): lax.all_to_all(spectra, ('fibre', 'seg'), split_axis=0, concat_axis=2, ti...  8.44 us
    another operation x1, other arithmetic, forward_table(): jnp.stack([(jnp.cos(angles) * scale).astype(jnp.bfloat16), (-jnp.sin(angl...  7.45 us
    all_to_all x1, starting transfers between devices, on_device(): lax.all_to_all(spans, 'fibre', split_axis=2, concat_axis=1, tiled=True)  6.35 us
  transfers between devices with their start and end apart: 5, of which 3 were waited for; matrix products, arithmetic and copies ran while one was open for 47% of the time, Pallas kernels for 0%

commit v1 on v0

--- a/solution.py
+++ b/solution.py
@@ -125,7 +125,10 @@
     sources = synthesize(
         lax.all_to_all(outgoing, ("fibre", "seg"), split_axis=2, concat_axis=0, tiled=True), table
     )
-    regrouped = lax.all_to_all(sources, "fibre", split_axis=0, concat_axis=1, tiled=True)
+    peers = lax.axis_size("fibre")
+    tiles = jnp.stack(jnp.split(sources, peers, axis=0), axis=0)
+    tiles = lax.all_to_all(tiles, "fibre", split_axis=0, concat_axis=0)
+    regrouped = jnp.concatenate(tiles, axis=1)
     return regrouped[None]
 
 

time: 164 us -> 164 us (level)
  no operation moved by 1% of the time
where the time goes in v1:
time: 164 us; the launch traced here: 163 us
  other arithmetic  50.7 us (31%)
  local copies, waits for them, and re-layouts  39.9 us (24%)
  starting transfers between devices  23 us (14%)
  waiting for transfers between devices  21.9 us (13%)
  blocking collectives  16.7 us (10%)
  matrix products  10.8 us (7%)
    convert_element_type x1, other arithmetic, forward_table(): (-jnp.sin(angles) * scale).astype(jnp.bfloat16)  35 us
    another operation x1, local copies, waits for them, and re-layouts, forward_table(): jnp.stack([(jnp.cos(angles) * scale).astype(jnp.bfloat16), (-jnp.sin(angl...  16.4 us
    all_to_all x1, blocking collectives, on_device(): tiles = lax.all_to_all(tiles, 'fibre', split_axis=0, concat_axis=0)  13.3 us
    reshape x1, local copies, waits for them, and re-layouts, synthesize(): table.reshape(2 * F, S)  13.1 us
    all_to_all x1, waiting for transfers between devices, on_device(): lax.all_to_all(adjoint_spec, ('fibre', 'seg'), split_axis=0, concat_axis=...  9.42 us
    all_to_all x1, waiting for transfers between devices, on_device(): lax.all_to_all(spectra, ('fibre', 'seg'), split_axis=0, concat_axis=2, ti...  8.44 us
    another operation x1, other arithmetic, forward_table(): jnp.stack([(jnp.cos(angles) * scale).astype(jnp.bfloat16), (-jnp.sin(angl...  7.45 us
    all_to_all x1, starting transfers between devices, on_device(): lax.all_to_all(spans, 'fibre', split_axis=2, concat_axis=1, tiled=True)  6.35 us
  transfers between devices with their start and end apart: 5, of which 3 were waited for; matrix products, arithmetic and copies ran while one was open for 47% of the time, Pallas kernels for 0%

profile of v1, /device:TPU:0, one launch (start us, length us, event | category | flops | bytes accessed | tf_op | source)
XLA Modules:
  0.0 163.2 jit_solution(5779909836414437357)
XLA Ops:
  0.0 1.8 %copy.56 = bf16[1,512,256]{1,2,0:T(8,128)(2,1)} copy(bf16[1,512,256]{2,1,0:T(8,128)(2,1)} %param.6) | data formatting | bytes 524288 | tf_op args[0]
  1.8 6.3 %all-to-all-start = ((bf16[1,512,4,64]{1,3,0,2:T(8,128)(2,1)}), bf16[1,512,4,64]{1,3,0,2:T(8,128)(2,1)S(1)}, u32[]{:S(2)}, u32[]{:S(2)}) async-start(bf16[1,512,4,64]{1,3,0,2:T(8,128)(2,1)} %bitcast.3), calls=%async_computation | async-start | bytes 524288 | tf_op jit(solution)/shard_map/all_to_all | solution.py:64
  8.1 35.0 %multiply_convert_fusion = (bf16[1024,1,2048]{2,0,1:T(8,128)(2,1)}, bf16[1024,1,2048]{2,0,1:T(8,128)(2,1)}) fusion(), kind=kLoop, calls=%fused_computation.10 | loop fusion | flops 39845888 | bytes 8388608 | tf_op jit(solution)/shard_map/convert_element_type | solution.py:22
  43.6 5.1 %convolution_convert_fusion.1 = bf16[1024,2,64]{0,2,1:T(8,128)(2,1)S(1)} fusion(bf16[2048,64,1]{0,1,2:T(8,128)(2,1)S(1)} %reshape.311, bf16[1024,1,2048]{2,0,1:T(8,128)(2,1)} %get-tuple-element.28, bf16[1024,1,2048]{2,0,1:T(8,128)(2,1)} %get-tuple-element.29), kind=kOutput, calls=%fused_computation.19 | convolution fusion | flops 541196288 | bytes 8912896 | tf_op jit(solution)/shard_map/qs,sn->qn/dot_general | solution.py:67
  49.1 1.1 reshape.316
  50.2 6.0 %all-to-all-start.1 = ((bf16[8,2,8192]{2,1,0:T(2,128)(2,1)}), bf16[8,2,8192]{2,1,0:T(2,128)(2,1)S(1)}, u32[]{:S(2)}, u32[]{:S(2)}) async-start(bf16[8,2,8192]{2,1,0:T(2,128)(2,1)} %reshape.316), calls=%async_computation.1 | async-start | bytes 524288 | tf_op jit(solution)/shard_map/all_to_all | solution.py:71
  56.3 8.4 %all-to-all-done.1 = bf16[8,2,8192]{2,1,0:T(2,128)(2,1)S(1)} async-done(((bf16[8,2,8192]{2,1,0:T(2,128)(2,1)}), bf16[8,2,8192]{2,1,0:T(2,128)(2,1)S(1)}, u32[]{:S(2)}, u32[]{:S(2)}) %all-to-all-start.1) | async-done | bytes 262176 | tf_op jit(solution)/shard_map/all_to_all | solution.py:71
  67.0 0.7 pad_maximum_fusion.4
  67.8 3.4 %all-to-all-start.2 = ((bf16[128,2,8,64]{0,3,1,2:T(8,128)(2,1)}), bf16[128,2,8,64]{0,3,1,2:T(8,128)(2,1)S(1)}, u32[]{:S(2)}, u32[]{:S(2)}) async-start(bf16[128,2,8,64]{0,3,1,2:T(8,128)(2,1)} %pad_maximum_fusion.4), calls=%async_computation.2 | async-start | bytes 524288 | tf_op jit(solution)/shard_map/all_to_all | solution.py:85
  71.2 4.5 %multiply_convert_fusion.3 = (bf16[1024,1,256]{2,0,1:T(8,128)(2,1)S(1)}, bf16[1024,1,256]{2,0,1:T(8,128)(2,1)S(1)}) fusion(s32[256]{0:T(256)S(1)} %and_select_fusion), kind=kLoop, calls=%fused_computation.30 | loop fusion | flops 4980736 | bytes 1049600 | tf_op jit(solution)/shard_map/convert_element_type | solution.py:36
  75.7 4.0 %all-to-all-done.2 = bf16[128,2,8,64]{0,3,1,2:T(8,128)(2,1)S(1)} async-done(((bf16[128,2,8,64]{0,3,1,2:T(8,128)(2,1)}), bf16[128,2,8,64]{0,3,1,2:T(8,128)(2,1)S(1)}, u32[]{:S(2)}, u32[]{:S(2)}) %all-to-all-start.2) | async-done | bytes 262176 | tf_op jit(solution)/shard_map/all_to_all | solution.py:85
  80.3 3.4 %psum.7 = bf16[2,32,256]{2,1,0:T(8,128)(2,1)S(1)} all-reduce(bf16[2,32,256]{2,1,0:T(8,128)(2,1)S(1)} %bitcast.123), channel_id=1, replica_groups=mesh['groups'=2,'fibre'=4,'seg'=2,'rec'=2] {'rec'}, use_global_device_ids=true, to_apply=%region_0.2 | all-reduce | flops 16384 | bytes 65536 | tf_op jit(solution)/shard_map/psum | solution.py:91
  84.6 1.1 reshape.318
  85.7 3.6 %all-to-all-start.3 = ((bf16[8,2,8192]{2,1,0:T(2,128)(2,1)}), bf16[8,2,8192]{2,1,0:T(2,128)(2,1)S(1)}, u32[]{:S(2)}, u32[]{:S(2)}) async-start(bf16[8,2,8192]{2,1,0:T(2,128)(2,1)} %reshape.318), calls=%async_computation.3 | async-start | bytes 524288 | tf_op jit(solution)/shard_map/all_to_all | solution.py:99
  89.3 9.4 %all-to-all-done.3 = bf16[8,2,8192]{2,1,0:T(2,128)(2,1)S(1)} async-done(((bf16[8,2,8192]{2,1,0:T(2,128)(2,1)}), bf16[8,2,8192]{2,1,0:T(2,128)(2,1)S(1)}, u32[]{:S(2)}, u32[]{:S(2)}) %all-to-all-start.3) | async-done | bytes 262176 | tf_op jit(solution)/shard_map/all_to_all | solution.py:99
  100.1 2.1 %scatter_fusion = f32[16,128,2,32]{1,3,2,0:T(8,128)S(1)} fusion(f32[16,128,2,32]{1,3,2,0:T(8,128)S(1)} %broadcast_in_dim.20, s32[32]{0:T(128)S(1)} %pad_add_fusion, f32[32,128,2,32]{1,3,2,0:T(8,128)S(1)} %maximum_bitcast_fusion), kind=kCustom, calls=%fused_computation.2 | custom fusion | flops 262144 | bytes 3145856 | tf_op jit(solution)/shard_map/scatter-add | solution.py:120
  102.3 0.7 copy.71
  103.1 3.6 %all-to-all-start.4 = ((bf16[128,2,8,64]{0,3,1,2:T(8,128)(2,1)}), bf16[128,2,8,64]{0,3,1,2:T(8,128)(2,1)S(1)}, u32[]{:S(2)}, u32[]{:S(2)}) async-start(bf16[128,2,8,64]{0,3,1,2:T(8,128)(2,1)} %copy.71), calls=%async_computation.4 | async-start | bytes 524288 | tf_op jit(solution)/shard_map/all_to_all | solution.py:126
  106.7 7.4 %pad_maximum_fusion = bf16[1024,2,2048]{2,0,1:T(8,128)(2,1)} fusion(bf16[1024,1,2048]{2,0,1:T(8,128)(2,1)} %get-tuple-element.28, bf16[1024,1,2048]{2,0,1:T(8,128)(2,1)} %get-tuple-element.29), kind=kLoop, calls=%fused_computation.9 | loop fusion | flops 4194304 | bytes 16777216 | tf_op jit(solution)/shard_map/stack | solution.py:19
  114.1 16.4 %copy.55 = bf16[1024,2,2048]{2,1,0:T(2,128)(2,1)} copy(bf16[1024,2,2048]{2,0,1:T(8,128)(2,1)} %pad_maximum_fusion) | data formatting | bytes 16777216 | tf_op jit(solution)/shard_map/stack | solution.py:19
  130.5 13.1 %reshape.266 = bf16[2048,2048]{1,0:T(8,128)(2,1)} reshape(bf16[1024,2,2048]{2,1,0:T(2,128)(2,1)} %copy.55) | data formatting | bytes 16777216 | tf_op jit(solution)/shard_map/reshape | solution.py:47
  144.1 5.0 %convolution_convert_fusion = bf16[2048,64]{0,1:T(8,128)(2,1)S(1)} fusion(bf16[2048,2048]{1,0:T(8,128)(2,1)} %reshape.266, bf16[2048,64]{1,0:T(8,128)(2,1)S(1)} %bitcast.110), kind=kOutput, calls=%fused_computation.15 | convolution fusion | flops 537001984 | bytes 8912896 | tf_op jit(solution)/shard_map/qn,qt->tn/dot_general | solution.py:46
  149.1 13.3 %all_to_all.74 = bf16[4,512,64]{1,2,0:T(8,128)(2,1)S(1)} all-to-all(bf16[4,512,64]{1,2,0:T(8,128)(2,1)S(1)} %pad_maximum_fusion.5), channel_id=1, replica_groups=mesh['groups'=2,'fibre'=4,'seg'=2,'rec'=2] {'fibre'}, dimensions={0} | all-to-all | bytes 524288 | tf_op jit(solution)/shard_map/all_to_all | solution.py:130
  162.4 0.8 copy.73
  (44 shorter events, 6.4 us)
Async XLA Ops:
  1.8 41.4 %all-to-all-start = ((bf16[1,512,4,64]{1,3,0,2:T(8,128)(2,1)}), bf16[1,512,4,64]{1,3,0,2:T(8,128)(2,1)S(1)}, u32[]{:S(2)}, u32[]{:S(2)}) async-start(bf16[1,512,4,64]{1,3,0,2:T(8,128)(2,1)} %bitcast.3), calls=%async_computation | async-start | bytes 524288 | tf_op jit(solution)/shard_map/all_to_all | solution.py:64
  43.6 12.6 %copy-start.2 = (s32[16,2]{0,1:T(2,128)S(1)}, s32[16,2]{0,1:T(2,128)}, u32[]{:S(2)}) copy-start(s32[16,2]{0,1:T(2,128)} %param.7) | copy-start | bytes 388
  48.7 22.5 %copy-start.1 = (s32[2,256]{1,0:T(2,128)S(1)}, s32[2,256]{1,0:T(2,128)}, u32[]{:S(2)}) copy-start(s32[2,256]{1,0:T(2,128)} %param.9) | copy-start | bytes 6148
  48.7 35.0 %copy-start = (f32[2,32,256]{2,1,0:T(8,128)S(1)}, f32[2,32,256]{2,1,0:T(8,128)}, u32[]{:S(2)}) copy-start(f32[2,32,256]{2,1,0:T(8,128)} %param.8) | copy-start | bytes 196612
  50.2 14.5 %all-to-all-start.1 = ((bf16[8,2,8192]{2,1,0:T(2,128)(2,1)}), bf16[8,2,8192]{2,1,0:T(2,128)(2,1)S(1)}, u32[]{:S(2)}, u32[]{:S(2)}) async-start(bf16[8,2,8192]{2,1,0:T(2,128)(2,1)} %reshape.316), calls=%async_computation.1 | async-start | bytes 524288 | tf_op jit(solution)/shard_map/all_to_all | solution.py:71
  67.8 12.0 %all-to-all-start.2 = ((bf16[128,2,8,64]{0,3,1,2:T(8,128)(2,1)}), bf16[128,2,8,64]{0,3,1,2:T(8,128)(2,1)S(1)}, u32[]{:S(2)}, u32[]{:S(2)}) async-start(bf16[128,2,8,64]{0,3,1,2:T(8,128)(2,1)} %pad_maximum_fusion.4), calls=%async_computation.2 | async-start | bytes 524288 | tf_op jit(solution)/shard_map/all_to_all | solution.py:85
  85.7 13.1 %all-to-all-start.3 = ((bf16[8,2,8192]{2,1,0:T(2,128)(2,1)}), bf16[8,2,8192]{2,1,0:T(2,128)(2,1)S(1)}, u32[]{:S(2)}, u32[]{:S(2)}) async-start(bf16[8,2,8192]{2,1,0:T(2,128)(2,1)} %reshape.318), calls=%async_computation.3 | async-start | bytes 524288 | tf_op jit(solution)/shard_map/all_to_all | solution.py:99
  103.1 40.6 %all-to-all-start.4 = ((bf16[128,2,8,64]{0,3,1,2:T(8,128)(2,1)}), bf16[128,2,8,64]{0,3,1,2:T(8,128)(2,1)S(1)}, u32[]{:S(2)}, u32[]{:S(2)}) async-start(bf16[128,2,8,64]{0,3,1,2:T(8,128)(2,1)} %copy.71), calls=%async_computation.4 | async-start | bytes 524288 | tf_op jit(solution)/shard_map/all_to_all | solution.py:126
